TPU v7x, 32 devices: a whole 2x2x4 slice. The times are simulated.
32 devices in a mesh: dom: 8 (over y, x, core), shift: 4 (over z).
Axes of the slice: x: 2, y: 2, z: 4, core: 2. Of those that a mesh axis runs over, the one named last changes fastest.
Arguments:
- sources: float32 [32, 32, 16, 128], P('shift', 'dom'), may hold values from -6 to 6
- kappa: float32 [32, 16, 128], P('dom'), may hold values from 0 to 2
- mass: float32 [32, 16, 128], P('dom'), may hold values from 0.25 to 4
- shift_table: float32 [64], replicated, may hold values from 0.5 to 4
- shift_ids: int32 [16], P('shift'), may hold values from 0 to 63
- sketch: bfloat16 [1024, 32, 16, 128], P(None, 'dom'), may hold values from -0.1875 to 0.1875
Outputs:
- solution: float32 [16, 32, 32, 16, 128], P('shift', None, 'dom')
- residual: float32 [16, 32, 32, 16, 128], P('shift', None, 'dom')
Inputs may be any that keep to these rules, and one draw needn't show every extreme that they name: `shift_ids`: index into shift_table.
All inputs are finite; a program needn't handle non-finite values.
Results may differ from a plain program's by a relative error of at most 0.0026.
Values sent between devices are 32-bit elements; how exact they have to be, the bound alone decides.
A program may use at most 128 MiB of HBM per device.

v0:
```python
import functools

import jax
import jax.numpy as jnp
from jax import lax
from jax.experimental import pallas as pl
from jax.experimental.pallas import tpu as pltpu
from jax.sharding import PartitionSpec as P

HALO = 3
PIECES = 2
LANES = 128
MID = 2.25
BASIS = 10
IMAGES = ((1, 2), (3, 4, 5), (6, 7, 8, 9))
PAIRS = [(i, k) for i in range(BASIS) for k in range(i, BASIS)]
PAIR_INDEX = {pair: n for n, pair in enumerate(PAIRS)}


def neighbour_sum(field):
    inner = field[1:-1]
    shape = inner.shape
    total = field[2:] + field[:-2]
    for dim in (1, 2):
        size = shape[dim]
        place = lax.broadcasted_iota(jnp.int32, shape, dim)
        total = total + jnp.where(place > 0, pltpu.roll(inner, 1, dim), 0.0)
        total = total + jnp.where(place < size - 1, pltpu.roll(inner, size - 1, dim), 0.0)
    return total


def plane_mask(shape, width, low, high):
    plane = lax.broadcasted_iota(jnp.int32, shape, 0)
    return jnp.where(plane < width, low, jnp.where(plane >= shape[0] - width, high, 1.0))


def edge_flags():
    me = lax.axis_index("dom")
    last = lax.axis_size("dom") - 1
    return (me > 0).astype(jnp.float32), (me < last).astype(jnp.float32)


def basis_fields(w0, diag, mass, mask1, mask2):
    sixth = 1.0 / 6.0
    center = 6.0 + MID
    d1, m1 = diag[1:-1], mass[1:-1]
    d2, m2 = diag[2:-2], mass[2:-2]
    d3, m3 = diag[3:-3], mass[3:-3]
    w0i = w0[1:-1]
    a0 = d1 * w0i - neighbour_sum(w0)
    a1 = m1 * w0i
    scaled1 = sixth * mask1
    g0 = (a0 - center * w0i) * scaled1
    g1 = (a1 - w0i) * scaled1
    g0i, g1i = g0[1:-1], g1[1:-1]
    b0 = d2 * g0i - neighbour_sum(g0)
    b1 = d2 * g1i - neighbour_sum(g1) + m2 * g0i
    b2 = m2 * g1i
    scaled2 = sixth * mask2
    h0 = (b0 - center * g0i) * scaled2
    h1 = (b1 - center * g1i - g0i) * scaled2
    h2 = (b2 - g1i) * scaled2
    h0i, h1i, h2i = h0[1:-1], h1[1:-1], h2[1:-1]
    e0 = d3 * h0i - neighbour_sum(h0)
    e1 = d3 * h1i - neighbour_sum(h1) + m3 * h0i
    e2 = d3 * h2i - neighbour_sum(h2) + m3 * h1i
    e3 = m3 * h2i
    return [
        w0[3:-3], a0[2:-2], a1[2:-2], b0[1:-1], b1[1:-1], b2[1:-1], e0, e1, e2, e3
    ]


def solve_small(h_vals, entry):
    l00 = jnp.sqrt(entry[0][0])
    l10 = entry[1][0] / l00
    l20 = entry[2][0] / l00
    l11 = jnp.sqrt(entry[1][1] - l10 * l10)
    l21 = (entry[2][1] - l20 * l10) / l11
    l22 = jnp.sqrt(entry[2][2] - l20 * l20 - l21 * l21)
    f0 = h_vals[0] / l00
    f1 = (h_vals[1] - l10 * f0) / l11
    f2 = (h_vals[2] - l20 * f0 - l21 * f1) / l22
    c2 = f2 / l22
    c1 = (f1 - l21 * c2) / l11
    c0 = (f0 - l10 * c1 - l20 * c2) / l00
    return (c0, c1, c2)


def coefficients(gram, tau):
    def product(left, right):
        by_degree = {}
        for p, i in enumerate(left):
            for q, k in enumerate(right):
                n = PAIR_INDEX[(min(i, k), max(i, k))]
                column = gram[:, n : n + 1]
                by_degree[p + q] = by_degree[p + q] + column if p + q in by_degree else column
        top = max(by_degree)
        total = jnp.broadcast_to(by_degree[top], (gram.shape[0], LANES))
        for degree in range(top - 1, -1, -1):
            total = total * tau + by_degree[degree]
        return total

    h_vals = [product(image, (0,)) for image in IMAGES]
    entry = [[None] * 3 for _ in range(3)]
    for i in range(3):
        for k in range(i + 1):
            entry[i][k] = product(IMAGES[i], IMAGES[k])
    ridge = 0.001 * (entry[0][0] + entry[1][1] + entry[2][2]) / 3.0 + 1.0
    for i in range(3):
        entry[i][i] = entry[i][i] + ridge
    return solve_small(h_vals, entry)


def project_kernel(
    n, groups, src_hbm, kappa_hbm, mass_hbm, table_ref, ids_ref, sketch_ref,
    wide_ref, coeff_ref, c_ref,
    src_ref, kappa_ref, mass_ref, mine_ref, rows_buf, raw_ref, fields_ref, out_buf, in_buf, gram_own, gram_in, gram_all,
    load_sem, in_sem, own_sem, own_send, own_recv, z_send, z_recv, halo_send, halo_recv, km_send, km_recv,
    rs_send, rs_recv, g_send, g_recv, s_send, s_recv,
):
    me = lax.axis_index("dom")
    group = lax.axis_index("shift")
    nb, slab = src_ref.shape[0], src_ref.shape[1]
    block = rows_buf.shape[1]
    columns = BASIS * nb
    right, left = lax.rem(me + 1, n), lax.rem(me + n - 1, n)
    has_right, has_left = me < n - 1, me > 0

    def remote(src, dst, send, recv, **where):
        return pltpu.make_async_remote_copy(
            src_ref=src, dst_ref=dst, send_sem=send, recv_sem=recv,
            device_id=where, device_id_type=pl.DeviceIdType.MESH,
        )

    def load(t):
        owner = lax.rem(me + 1 + t, n)
        return pltpu.make_async_copy(
            sketch_ref.at[pl.ds(owner * block, block)], rows_buf.at[t], load_sem.at[t]
        )

    barrier = pltpu.get_barrier_semaphore()
    for t in range(1, n):
        pl.semaphore_signal(
            barrier, inc=1, device_id={"dom": lax.rem(me + t, n)},
            device_id_type=pl.DeviceIdType.MESH,
        )
    for t in range(1, groups):
        pl.semaphore_signal(
            barrier, inc=1, device_id={"shift": lax.rem(group + t, groups)},
            device_id_type=pl.DeviceIdType.MESH,
        )
    arguments = [
        pltpu.make_async_copy(src_hbm, src_ref, in_sem.at[0]),
        pltpu.make_async_copy(kappa_hbm, kappa_ref, in_sem.at[1]),
        pltpu.make_async_copy(mass_hbm, mass_ref, in_sem.at[2]),
    ]
    for copy in arguments:
        copy.start()
    for t in range(n):
        load(t).start()
    for copy in arguments:
        copy.wait()
    pl.semaphore_wait(barrier, n - 1 + groups - 1)

    def sides(side):
        if side == 0:
            return slab - HALO, pl.ds(0, HALO), right
        return 0, pl.ds(slab + HALO, HALO), left

    def own_halo(side):
        first, target, there = sides(side)
        return remote(
            src_ref.at[:, pl.ds(first, HALO)], mine_ref.at[:, target],
            own_send.at[side], own_recv.at[side], dom=there,
        )

    hops = []
    for k in range(1, groups // 2 + 1):
        for way in range(2):
            parts = (0, nb)
            if 2 * k == groups:
                parts = ((0, nb // 2), (nb // 2, nb - nb // 2))[way]
            hops.append((way, k, pl.ds(*parts)))

    def shifted(way, k):
        step = k if way == 0 else groups - k
        return lax.rem(group + step, groups)

    def across(hop):
        way, k, part = hop
        if k == 1:
            slot, src = group, src_ref.at[part]
        else:
            slot = shifted(1 - way, k - 1)
            src = wide_ref.at[slot, part, pl.ds(HALO, slab)]
        return remote(
            src, wide_ref.at[slot, part, pl.ds(HALO, slab)],
            z_send.at[way, k - 1], z_recv.at[way, k - 1], shift=shifted(way, 1),
        )

    def halo(hop, side):
        way, k, part = hop
        slot = shifted(1 - way, k)
        first, target, there = sides(side)
        return remote(
            wide_ref.at[slot, part, pl.ds(HALO + first, HALO)], wide_ref.at[slot, part, target],
            halo_send.at[way, k - 1, side], halo_recv.at[way, k - 1, side], dom=there,
        )

    def coeff_halo(which, side):
        ref = (kappa_ref, mass_ref)[which]
        first, target, there = sides(side)
        return remote(
            ref.at[pl.ds(first, HALO)], coeff_ref.at[which, target], km_send.at[which, side],
            km_recv.at[which, side], dom=there,
        )

    @pl.when(has_right)
    def _():
        own_halo(0).start()
        for which in range(2):
            coeff_halo(which, 0).start()

    @pl.when(has_left)
    def _():
        own_halo(1).start()
        for which in range(2):
            coeff_halo(which, 1).start()

    for hop in hops:
        if hop[1] == 1:
            across(hop).start()

    mine_ref[:, pl.ds(HALO, slab)] = src_ref[...]
    coeff_ref[0, pl.ds(HALO, slab)] = kappa_ref[...]
    coeff_ref[1, pl.ds(HALO, slab)] = mass_ref[...]

    @pl.when(jnp.logical_not(has_left))
    def _():
        mine_ref[:, pl.ds(0, HALO)] = jnp.zeros(
            (nb, HALO) + src_ref.shape[2:], jnp.float32
        )
        coeff_ref[:, pl.ds(0, HALO)] = jnp.zeros((2, HALO) + src_ref.shape[2:], jnp.float32)

    @pl.when(jnp.logical_not(has_right))
    def _():
        mine_ref[:, pl.ds(slab + HALO, HALO)] = jnp.zeros(
            (nb, HALO) + src_ref.shape[2:], jnp.float32
        )
        coeff_ref[:, pl.ds(slab + HALO, HALO)] = jnp.zeros(
            (2, HALO) + src_ref.shape[2:], jnp.float32
        )

    @pl.when(has_left)
    def _():
        own_halo(0).wait_recv()
        for which in range(2):
            coeff_halo(which, 0).wait_recv()

    @pl.when(has_right)
    def _():
        own_halo(1).wait_recv()
        for which in range(2):
            coeff_halo(which, 1).wait_recv()

    keep = pltpu.make_async_copy(mine_ref, wide_ref.at[group], own_sem)
    keep.start()
    low, high = edge_flags()
    mass = coeff_ref[1]
    diag = (6.0 - coeff_ref[0]) + MID * mass
    planes = slab + 2 * HALO
    grid_tail = src_ref.shape[2:]
    mask1 = plane_mask((planes - 2,) + grid_tail, 2, low, high)
    mask2 = plane_mask((planes - 4,) + grid_tail, 1, low, high)

    def one_source(b, carry):
        fields = basis_fields(mine_ref[b], diag, mass, mask1, mask2)
        for k, field in enumerate(fields):
            rounded = field.astype(jnp.bfloat16)
            raw_ref[k * nb + b] = rounded
            raw_ref[columns + k * nb + b] = (field - rounded.astype(jnp.float32)).astype(
                jnp.bfloat16
            )
        return carry

    lax.fori_loop(0, nb, one_source, 0)
    fields_ref[...] = raw_ref[...].reshape(fields_ref.shape)

    def forward(hop):
        across(hop).wait_recv()
        for later in hops:
            if later[0] == hop[0] and later[1] == hop[1] + 1:
                across(later).start()

        @pl.when(has_right)
        def _():
            halo(hop, 0).start()

        @pl.when(has_left)
        def _():
            halo(hop, 1).start()

    early = [hop for hop in hops if hop[1] < groups // 2]
    late = [hop for hop in hops if hop[1] == groups // 2]
    def scatter(t):
        return remote(
            out_buf.at[t], in_buf.at[t], rs_send.at[t], rs_recv.at[t],
            dom=lax.rem(me + 1 + t, n),
        )

    per = next(size for size in (PIECES, 2, 1) if n % size == 0)

    def multiply(u):
        for t in range(per):
            load(u * per + t).wait()
        product = lax.dot_general(
            rows_buf[pl.ds(u * per, per)].reshape(per * block, fields_ref.shape[1]),
            fields_ref[...], (((1,), (1,)), ((), ())), preferred_element_type=jnp.float32,
        )
        turned = product.T
        summed = turned[:columns] + turned[columns:]
        return [summed[:, t * block : (t + 1) * block] for t in range(per)]

    def send(t, piece):
        out_buf[t] = piece
        scatter(t).start()

    def step(u, carry):
        for t, piece in enumerate(multiply(u)):
            send(u * per + t, piece)
        return carry

    lax.fori_loop(0, n // per - 1, step, 0)
    pieces = multiply(n // per - 1)
    for t in range(per - 1):
        send(n - per + t, pieces[t])
    total = pieces[per - 1]
    for hop in early:
        forward(hop)

    for t in range(n - 1):
        scatter(t).wait_recv()
        total = total + in_buf[t]

    lane = lax.broadcasted_iota(jnp.int32, (nb, LANES), 1)
    gram = jnp.zeros((nb, LANES), jnp.float32)
    for p, (i, k) in enumerate(PAIRS):
        value = jnp.sum(
            total[i * nb : (i + 1) * nb] * total[k * nb : (k + 1) * nb], axis=1, keepdims=True
        )
        gram = jnp.where(lane == p, value, gram)
    gram_own[...] = gram

    def share(t):
        return remote(
            gram_own, gram_in.at[t - 1], g_send.at[t - 1], g_recv.at[t - 1],
            dom=lax.rem(me + t, n),
        )

    for t in range(1, n):
        share(t).start()
    for t in range(1, n):
        share(t).wait_recv()
        gram = gram + gram_in[t - 1]
    gram_all[group] = gram
    for hop in late:
        forward(hop)

    def spread(t):
        return remote(
            gram_all.at[group], gram_all.at[group], s_send.at[t - 1], s_recv.at[t - 1],
            shift=lax.rem(group + t, groups),
        )

    for t in range(1, groups):
        spread(t).start()
    tau = jnp.zeros((1, LANES), jnp.float32)
    lane_row = lax.broadcasted_iota(jnp.int32, (1, LANES), 1)
    for j in range(ids_ref.shape[0]):
        tau = jnp.where(lane_row == j, table_ref[ids_ref[j]] - MID, tau)
    for t in range(1, groups):
        spread(t).wait_recv()
    count = groups * nb
    solved = coefficients(gram_all[...].reshape(count, LANES), tau)
    shifts = ids_ref.shape[0]
    packed = jnp.zeros((count, LANES), jnp.float32)
    lane_count = lax.broadcasted_iota(jnp.int32, (count, LANES), 1)
    for i in range(3):
        value = jnp.where(lane_count < shifts, solved[i], 0.0)
        packed = packed + (pltpu.roll(value, i * shifts, 1) if i else value)
    c_ref[...] = packed

    for hop in hops:
        @pl.when(has_left)
        def _():
            halo(hop, 0).wait_recv()

        @pl.when(has_right)
        def _():
            halo(hop, 1).wait_recv()

    keep.wait()

    @pl.when(has_right)
    def _():
        own_halo(0).wait_send()
        for hop in hops:
            halo(hop, 0).wait_send()
        for which in range(2):
            coeff_halo(which, 0).wait_send()

    @pl.when(has_left)
    def _():
        own_halo(1).wait_send()
        for hop in hops:
            halo(hop, 1).wait_send()
        for which in range(2):
            coeff_halo(which, 1).wait_send()

    for t in range(1, groups):
        spread(t).wait_send()
    for hop in hops:
        across(hop).wait_send()
    for t in range(n - 1):
        scatter(t).wait_send()
    for t in range(1, n):
        share(t).wait_send()


def combine_kernel(wide_ref, coeff_ref, c_ref, table_ref, ids_ref, sol_ref, res_ref, step_ref):
    batch, planes = wide_ref.shape[0], wide_ref.shape[1]
    me = lax.axis_index("dom")
    has_low, has_high = me > 0, me < lax.axis_size("dom") - 1
    shifts = ids_ref.shape[0]
    first = pl.program_id(0) * batch

    def inside(field, width):
        return jnp.concatenate(
            [
                jnp.where(has_low, field[:width], 0.0),
                field[width:-width],
                jnp.where(has_high, field[-width:], 0.0),
            ],
            axis=0,
        )

    @pl.when(pl.program_id(0) == 0)
    def _():
        for j in range(shifts):
            sigma = table_ref[ids_ref[j]]
            step_ref[j] = sigma * (coeff_ref[1, 1:-1] - 1.0) - coeff_ref[0, 1:-1]

    def one_source(i, carry):
        w0 = inside(wide_ref[i], HALO)
        own = w0[3:-3]
        near = neighbour_sum(w0)
        b = first + i
        for j in range(shifts):
            center = 6.0 + table_ref[ids_ref[j]]
            v1 = inside(step_ref[j] * w0[1:-1] - near, 2)
            v2 = inside(step_ref[j, 1:-1] * v1[1:-1] - neighbour_sum(v1), 1)
            v3 = step_ref[j, 2:-2] * v2[1:-1] - neighbour_sum(v2)
            v1, v2 = v1[2:-2], v2[1:-1]
            c0 = c_ref[b, j]
            c1 = c_ref[b, shifts + j] * (1.0 / 6.0)
            c2 = c_ref[b, 2 * shifts + j] * (1.0 / 36.0)
            sol_ref[j, i] = c0 * own + c1 * v1 + c2 * v2
            res_ref[j, i] = (
                (1.0 - c0 * center) * own - (c0 + c1 * center) * v1
                - (c1 + c2 * center) * v2 - c2 * v3
            )
        return carry

    lax.fori_loop(0, batch, one_source, 0)


def on_device(sources, kappa, mass, shift_table, shift_ids, sketch):
    n, groups = lax.axis_size("dom"), lax.axis_size("shift")
    nb, slab = sources.shape[0], sources.shape[1]
    tail = sources.shape[2:]
    shifts = shift_ids.shape[0]
    rows = sketch.shape[0]
    block = rows // n
    cells = slab * tail[0] * tail[1]
    planes = slab + 2 * HALO
    count = groups * nb
    columns = BASIS * nb
    vmem = pl.BlockSpec(memory_space=pltpu.VMEM)
    hbm = pl.BlockSpec(memory_space=pl.ANY)
    smem = pl.BlockSpec(memory_space=pltpu.SMEM)
    dma = pltpu.SemaphoreType.DMA
    f32 = jnp.float32
    wide, coeff, solved = pl.pallas_call(
        functools.partial(project_kernel, n, groups),
        out_shape=(
            jax.ShapeDtypeStruct((groups, nb, planes) + tail, f32),
            jax.ShapeDtypeStruct((2, planes) + tail, f32),
            jax.ShapeDtypeStruct((count, LANES), f32),
        ),
        in_specs=[hbm, hbm, hbm, smem, smem, hbm],
        out_specs=(hbm, vmem, vmem),
        scratch_shapes=[
            pltpu.VMEM(sources.shape, f32),
            pltpu.VMEM(kappa.shape, f32),
            pltpu.VMEM(mass.shape, f32),
            pltpu.VMEM((nb, planes) + tail, f32),
            pltpu.VMEM((n, block, slab) + tail, jnp.bfloat16),
            pltpu.VMEM((2 * columns, slab) + tail, jnp.bfloat16),
            pltpu.VMEM((2 * columns, cells), jnp.bfloat16),
            pltpu.VMEM((n - 1, columns, block), f32),
            pltpu.VMEM((n - 1, columns, block), f32),
            pltpu.VMEM((nb, LANES), f32),
            pltpu.VMEM((n - 1, nb, LANES), f32),
            pltpu.VMEM((groups, nb, LANES), f32),
            dma((n,)),
            dma((3,)), dma,
            dma((2,)), dma((2,)),
            dma((2, groups // 2)), dma((2, groups // 2)),
            dma((2, groups // 2, 2)), dma((2, groups // 2, 2)),
            dma((2, 2)), dma((2, 2)),
            dma((n - 1,)), dma((n - 1,)),
            dma((n - 1,)), dma((n - 1,)),
            dma((groups - 1,)), dma((groups - 1,)),
        ],
        compiler_params=pltpu.CompilerParams(
            collective_id=0, has_side_effects=True, vmem_limit_bytes=56 << 20
        ),
        name="project",
    )(sources, kappa, mass, shift_table, shift_ids, sketch)

    batch = 4 if count % 4 == 0 else 1
    out = jax.ShapeDtypeStruct((shifts, count, slab) + tail, f32)
    out_spec = pl.BlockSpec((shifts, batch, slab) + tail, lambda i: (0, i, 0, 0, 0))
    return pl.pallas_call(
        combine_kernel,
        grid=(count // batch,),
        out_shape=(out, out),
        in_specs=[
            pl.BlockSpec((batch, planes) + tail, lambda i: (i, 0, 0, 0)),
            pl.BlockSpec((2, planes) + tail, lambda i: (0, 0, 0, 0)),
            smem, smem, smem,
        ],
        out_specs=(out_spec, out_spec),
        scratch_shapes=[pltpu.VMEM((shifts, planes - 2) + tail, f32)],
        compiler_params=pltpu.CompilerParams(vmem_limit_bytes=63 << 20),
        name="combine",
    )(wide.reshape((count, planes) + tail), coeff, solved, shift_table, shift_ids)


def solution(mesh):
    placed = (
        P("shift", "dom", None, None),
        P("dom", None, None),
        P("dom", None, None),
        P(),
        P("shift"),
        P(None, "dom", None, None),
    )
    return jax.shard_map(
        on_device,
        mesh=mesh,
        in_specs=placed,
        out_specs=(P("shift", None, "dom", None, None), P("shift", None, "dom", None, None)),
        check_vma=False,
    )
```

profile of v0, /device:TPU:1, one launch (start us, length us, event | category | flops | bytes accessed | tf_op | source)
XLA Modules:
  0.0 59.0 jit_solution(1786756697881506854)
XLA Ops:
  0.6 43.4 %project.1 = (f32[4,8,10,16,128]{4,3,2,1,0:T(8,128)}, f32[2,10,16,128]{3,2,1,0:T(8,128)}, f32[32,128]{1,0:T(8,128)}) custom-call(f32[8,4,16,128]{3,2,1,0:T(8,128)} %src_hbm.1, f32[4,16,128]{2,1,0:T(8,128)} %kappa_hbm.1, f32[4,16,128]{2,1,0:T(8,128)} %mass_hbm.1, f32[64]{0:T(128)} %table_ref.3, s32[4]{0:T(128)} %ids_ref.3, bf16[1024,4,16,128]{3,2,1,0:T(8,128)(2,1)} %sketch_ref.1), custom_call_target="tpu_custom_call" | custom-call | tf_op jit(solution)/shard_map/project/pallas_call | solution.py:493
  44.0 14.9 %combine.1 = (f32[4,32,4,16,128]{4,3,2,1,0:T(8,128)}, f32[4,32,4,16,128]{4,3,2,1,0:T(8,128)}) custom-call(f32[32,10,16,128]{3,2,1,0:T(8,128)} %bitcast.1, f32[2,10,16,128]{3,2,1,0:T(8,128)} %get-tuple-element.6.coeff_ref, f32[32,128]{1,0:T(8,128)} %get-tuple-element.7.c_ref, f32[64]{0:T(128)} %table_ref.3, s32[4]{0:T(128)} %ids_ref.3), custom_call_target="tpu_custom_call" | custom-call | tf_op jit(solution)/shard_map/combine/pallas_call | solution.py:534
where the time goes:
time: 59.1 us; the launch traced here: 59 us
  Pallas kernels  58.3 us (99%)
  between operations  0.64 us (1%)
    pallas_call x1, Pallas kernels, on_device(): pl.pallas_call(functools.partial(project_kernel, n, groups), out_shape=(j...  43.4 us
    pallas_call x1, Pallas kernels, on_device(): pl.pallas_call(combine_kernel, grid=(count // batch,), out_shape=(out, ou...  14.9 us

commit v1 on v0

v1 whole, which is shorter than its diff:
```python
import functools

import jax
import jax.numpy as jnp
from jax import lax
from jax.experimental import pallas as pl
from jax.experimental.pallas import tpu as pltpu
from jax.sharding import PartitionSpec as P

HALO = 3
STEPS = 4
LANES = 128
MID = 2.25
BASIS = 10
WEIGHTS = 6
IMAGES = ((1, 2), (3, 4, 5), (6, 7, 8, 9))
PAIRS = [(i, k) for i in range(BASIS) for k in range(i, BASIS)]
PAIR_INDEX = {pair: n for n, pair in enumerate(PAIRS)}


def neighbour_sum(field):
    inner = field[1:-1]
    shape = inner.shape
    total = field[2:] + field[:-2]
    for dim in (1, 2):
        size = shape[dim]
        place = lax.broadcasted_iota(jnp.int32, shape, dim)
        total = total + jnp.where(place > 0, pltpu.roll(inner, 1, dim), 0.0)
        total = total + jnp.where(place < size - 1, pltpu.roll(inner, size - 1, dim), 0.0)
    return total


def plane_mask(shape, width, low, high):
    plane = lax.broadcasted_iota(jnp.int32, shape, 0)
    return jnp.where(plane < width, low, jnp.where(plane >= shape[0] - width, high, 1.0))


def edge_flags():
    me = lax.axis_index("dom")
    last = lax.axis_size("dom") - 1
    return (me > 0).astype(jnp.float32), (me < last).astype(jnp.float32)


def basis_fields(w0, diag, mass, mask1, mask2):
    sixth = 1.0 / 6.0
    center = 6.0 + MID
    d1, m1 = diag[1:-1], mass[1:-1]
    d2, m2 = diag[2:-2], mass[2:-2]
    d3, m3 = diag[3:-3], mass[3:-3]
    w0i = w0[1:-1]
    a0 = d1 * w0i - neighbour_sum(w0)
    a1 = m1 * w0i
    scaled1 = sixth * mask1
    g0 = (a0 - center * w0i) * scaled1
    g1 = (a1 - w0i) * scaled1
    g0i, g1i = g0[1:-1], g1[1:-1]
    b0 = d2 * g0i - neighbour_sum(g0)
    b1 = d2 * g1i - neighbour_sum(g1) + m2 * g0i
    b2 = m2 * g1i
    scaled2 = sixth * mask2
    h0 = (b0 - center * g0i) * scaled2
    h1 = (b1 - center * g1i - g0i) * scaled2
    h2 = (b2 - g1i) * scaled2
    h0i, h1i, h2i = h0[1:-1], h1[1:-1], h2[1:-1]
    e0 = d3 * h0i - neighbour_sum(h0)
    e1 = d3 * h1i - neighbour_sum(h1) + m3 * h0i
    e2 = d3 * h2i - neighbour_sum(h2) + m3 * h1i
    e3 = m3 * h2i
    return [
        w0[3:-3], a0[2:-2], a1[2:-2], b0[1:-1], b1[1:-1], b2[1:-1], e0, e1, e2, e3
    ]


def solve_small(h_vals, entry):
    l00 = jnp.sqrt(entry[0][0])
    l10 = entry[1][0] / l00
    l20 = entry[2][0] / l00
    l11 = jnp.sqrt(entry[1][1] - l10 * l10)
    l21 = (entry[2][1] - l20 * l10) / l11
    l22 = jnp.sqrt(entry[2][2] - l20 * l20 - l21 * l21)
    f0 = h_vals[0] / l00
    f1 = (h_vals[1] - l10 * f0) / l11
    f2 = (h_vals[2] - l20 * f0 - l21 * f1) / l22
    c2 = f2 / l22
    c1 = (f1 - l21 * c2) / l11
    c0 = (f0 - l10 * c1 - l20 * c2) / l00
    return (c0, c1, c2)


def coefficients(gram, tau):
    def product(left, right):
        by_degree = {}
        for p, i in enumerate(left):
            for q, k in enumerate(right):
                n = PAIR_INDEX[(min(i, k), max(i, k))]
                column = gram[:, n : n + 1]
                by_degree[p + q] = by_degree[p + q] + column if p + q in by_degree else column
        top = max(by_degree)
        total = jnp.broadcast_to(by_degree[top], (gram.shape[0], LANES))
        for degree in range(top - 1, -1, -1):
            total = total * tau + by_degree[degree]
        return total

    h_vals = [product(image, (0,)) for image in IMAGES]
    entry = [[None] * 3 for _ in range(3)]
    for i in range(3):
        for k in range(i + 1):
            entry[i][k] = product(IMAGES[i], IMAGES[k])
    ridge = 0.001 * (entry[0][0] + entry[1][1] + entry[2][2]) / 3.0 + 1.0
    for i in range(3):
        entry[i][i] = entry[i][i] + ridge
    return solve_small(h_vals, entry)


def weights(solved, tau):
    c0, c1, c2 = solved
    shifted = 6.0 + MID + tau
    of_z1 = c2 * (1.0 / 6.0)
    of_z0 = (c1 - of_z1 * shifted) * (1.0 / 6.0)
    of_w0 = c0 - of_z0 * shifted
    return (of_w0, of_z0, of_z1, c0, c1, c2)


def project_kernel(
    n, groups, src_hbm, kappa_hbm, mass_hbm, table_ref, ids_ref, sketch_ref,
    image_ref, c_ref,
    wide_ref, coeff_ref, rows_buf, mat_ref, raw_ref, fields_ref, out_buf, in_buf, total_ref, gram_all,
    gram_rows, load_sem, in_sem, z_send, z_recv, halo_send, halo_recv, km_send, km_recv,
    rs_send, rs_recv, g_send, g_recv,
):
    me = lax.axis_index("dom")
    group = lax.axis_index("shift")
    nb = wide_ref.shape[1]
    slab = wide_ref.shape[2] - 2 * HALO
    tail = wide_ref.shape[3:]
    shifts = ids_ref.shape[0]
    columns = BASIS * nb
    rows = mat_ref.shape[0]
    blocks, block = rows_buf.shape[0], rows_buf.shape[1]
    steps = out_buf.shape[0]
    stride = rows // steps
    parts = stride // LANES
    chunk = rows // (n // nb)
    turns = chunk // stride
    right, left = lax.rem(me + 1, n), lax.rem(me + n - 1, n)
    has_right, has_left = me < n - 1, me > 0
    has_up, has_down = group < groups - 1, group > 0
    upper = (2 * group) // groups
    nearer = group + upper * (groups - 1 - 2 * group)

    def remote(src, dst, send, recv, **where):
        return pltpu.make_async_remote_copy(
            src_ref=src, dst_ref=dst, send_sem=send, recv_sem=recv,
            device_id=where, device_id_type=pl.DeviceIdType.MESH,
        )

    def load(t):
        return pltpu.make_async_copy(
            sketch_ref.at[pl.ds(t * block, block)], rows_buf.at[t], load_sem.at[t]
        )

    barrier = pltpu.get_barrier_semaphore()
    for t in range(1, n):
        pl.semaphore_signal(
            barrier, inc=1, device_id={"dom": lax.rem(me + t, n)},
            device_id_type=pl.DeviceIdType.MESH,
        )
    for t in range(1, groups):
        pl.semaphore_signal(
            barrier, inc=1, device_id={"shift": lax.rem(group + t, groups)},
            device_id_type=pl.DeviceIdType.MESH,
        )
    inner = pl.ds(HALO, slab)
    arguments = [
        pltpu.make_async_copy(src_hbm, wide_ref.at[group, :, inner], in_sem.at[0]),
        pltpu.make_async_copy(kappa_hbm, coeff_ref.at[0, inner], in_sem.at[1]),
        pltpu.make_async_copy(mass_hbm, coeff_ref.at[1, inner], in_sem.at[2]),
    ]
    for copy in arguments:
        copy.start()
    for t in range(blocks):
        load(t).start()

    @pl.when(jnp.logical_not(has_left))
    def _():
        wide_ref[:, :, pl.ds(0, HALO)] = jnp.zeros((groups, nb, HALO) + tail, jnp.float32)
        coeff_ref[:, pl.ds(0, HALO)] = jnp.zeros((2, HALO) + tail, jnp.float32)

    @pl.when(jnp.logical_not(has_right))
    def _():
        wide_ref[:, :, pl.ds(slab + HALO, HALO)] = jnp.zeros(
            (groups, nb, HALO) + tail, jnp.float32
        )
        coeff_ref[:, pl.ds(slab + HALO, HALO)] = jnp.zeros((2, HALO) + tail, jnp.float32)

    for copy in arguments:
        copy.wait()
    pl.semaphore_wait(barrier, n - 1 + groups - 1)

    def sides(side):
        if side == 0:
            return pl.ds(slab, HALO), pl.ds(0, HALO), right
        return pl.ds(HALO, HALO), pl.ds(slab + HALO, HALO), left

    def halo(slot, side):
        first, target, there = sides(side)
        return remote(
            wide_ref.at[slot, :, first], wide_ref.at[slot, :, target],
            halo_send.at[slot, side], halo_recv.at[slot, side], dom=there,
        )

    def coeff_halo(which, side):
        first, target, there = sides(side)
        return remote(
            coeff_ref.at[which, first], coeff_ref.at[which, target], km_send.at[which, side],
            km_recv.at[which, side], dom=there,
        )

    def across(slot, way):
        return remote(
            wide_ref.at[slot, :, inner], wide_ref.at[slot, :, inner],
            z_send.at[slot, way], z_recv.at[slot],
            shift=group + 1 - 2 * way,
        )

    def other(i):
        if i == 0:
            return group
        longer = 1 - 2 * upper
        both = (2 * nearer - i + groups) // groups
        swing = longer * ((i + 1) // 2) * (1 if i % 2 else -1)
        return group + both * swing + (1 - both) * longer * (i - nearer)

    def to_right(act):
        pl.when(has_right)(act)

    def to_left(act):
        pl.when(has_left)(act)

    def up_from(slot):
        return jnp.logical_and(slot <= group, has_up)

    def down_from(slot):
        return jnp.logical_and(slot >= group, has_down)

    @pl.when(has_right)
    def _():
        halo(group, 0).start()
        for which in range(2):
            coeff_halo(which, 0).start()

    @pl.when(has_left)
    def _():
        halo(group, 1).start()
        for which in range(2):
            coeff_halo(which, 1).start()

    @pl.when(has_up)
    def _():
        across(group, 0).start()

    @pl.when(has_down)
    def _():
        across(group, 1).start()

    def settle(t, carry):
        load(t).wait()
        mat_ref[pl.ds(pl.multiple_of(t * block, block), block)] = rows_buf[t].reshape(
            block, mat_ref.shape[1]
        )
        return carry

    lax.fori_loop(0, blocks, settle, 0)

    @pl.when(has_left)
    def _():
        halo(group, 0).wait_recv()
        for which in range(2):
            coeff_halo(which, 0).wait_recv()

    @pl.when(has_right)
    def _():
        halo(group, 1).wait_recv()
        for which in range(2):
            coeff_halo(which, 1).wait_recv()

    def forward(i):
        slot = other(i)
        across(slot, 0).wait_recv()

        @pl.when(up_from(slot))
        def _():
            across(slot, 0).start()

        @pl.when(down_from(slot))
        def _():
            across(slot, 1).start()

        @pl.when(has_right)
        def _():
            halo(slot, 0).start()

        @pl.when(has_left)
        def _():
            halo(slot, 1).start()

    def settled(i):
        slot = other(i)

        @pl.when(has_left)
        def _():
            halo(slot, 0).wait_recv()

        @pl.when(has_right)
        def _():
            halo(slot, 1).wait_recv()

    low, high = edge_flags()
    planes = slab + 2 * HALO

    def basis_of(slot, b):
        mass = coeff_ref[1]
        diag = (6.0 - coeff_ref[0]) + MID * mass
        mask1 = plane_mask((planes - 2,) + tail, 2, low, high)
        mask2 = plane_mask((planes - 4,) + tail, 1, low, high)
        return basis_fields(wide_ref[slot, b], diag, mass, mask1, mask2)

    def one_source(b, carry):
        for k, field in enumerate(basis_of(group, b)):
            rounded = field.astype(jnp.bfloat16)
            raw_ref[b * BASIS + k] = rounded
            raw_ref[columns + b * BASIS + k] = (field - rounded.astype(jnp.float32)).astype(
                jnp.bfloat16
            )
        return carry

    lax.fori_loop(0, nb, one_source, 0)
    fields_ref[...] = raw_ref[...].reshape(fields_ref.shape)

    def images_of(slot):
        def one(b, carry):
            w0, a0, a1, b0, b1, b2, e0, e1, e2, e3 = basis_of(slot, b)
            place = slot * nb + b
            image_ref[0, place] = w0
            for j in range(shifts):
                tau = table_ref[ids_ref[j]] - MID
                image_ref[1 + j, place] = a0 + tau * a1
                image_ref[1 + shifts + j, place] = b0 + tau * (b1 + tau * b2)
                image_ref[1 + 2 * shifts + j, place] = e0 + tau * (e1 + tau * (e2 + tau * e3))
            return carry

        lax.fori_loop(0, nb, one, 0)

    def scatter(u, there):
        turn = lax.rem(u, turns)
        return remote(
            out_buf.at[u, pl.ds(lax.rem(there, nb) * BASIS, BASIS)],
            in_buf.at[me, :, pl.ds(turn * parts, parts)],
            rs_send.at[u, lax.rem(there, nb)], rs_recv.at[me, turn], dom=there,
        )

    def gathered(source, turn):
        return remote(
            out_buf.at[turn, pl.ds(0, BASIS)],
            in_buf.at[source, :, pl.ds(turn * parts, parts)],
            rs_send.at[turn, 0], rs_recv.at[source, turn], dom=source,
        )

    def each_target(u, act):
        base = (u // turns) * nb
        for t in range(1, nb + 1):
            there = base + lax.rem(me + t, nb)

            @pl.when(there != me)
            def _(there=there):
                act(scatter(u, there))

    def step(u, carry):
        product = lax.dot_general(
            mat_ref[pl.ds(pl.multiple_of(u * stride, stride), stride)],
            fields_ref[...], (((1,), (1,)), ((), ())), preferred_element_type=jnp.float32,
        )
        turned = product.T
        summed = turned[:columns] + turned[columns:]
        for part in range(parts):
            out_buf[u, :, part, 0, :] = summed[:, part * LANES : (part + 1) * LANES]
        each_target(u, lambda copy: copy.start())
        return carry

    lax.fori_loop(0, steps, step, 0)
    forward(1)
    images_of(group)

    first_turn = (me // nb) * turns
    mine = pl.ds(lax.rem(me, nb) * BASIS, BASIS)
    for turn in range(turns):
        in_buf[me, :, pl.ds(turn * parts, parts)] = out_buf[first_turn + turn, mine]
    for t in range(1, n):
        for turn in range(turns):
            gathered(lax.rem(me + t, n), turn).wait_recv()
    for k in range(BASIS):
        summed = in_buf[0, k]
        for source in range(1, n):
            summed = summed + in_buf[source, k]
        total_ref[k] = summed.reshape(total_ref.shape[1:])
    lane = lax.broadcasted_iota(jnp.int32, total_ref.shape[1:], 1)
    gram = jnp.zeros(total_ref.shape[1:], jnp.float32)
    for p, (i, k) in enumerate(PAIRS):
        value = jnp.sum(total_ref[i] * total_ref[k], axis=1, keepdims=True)
        gram = jnp.where(lane == p, value, gram)
    own = group * n + me
    gram_all[own] = jnp.sum(gram, axis=0, keepdims=True)

    def share(dz, dd):
        return remote(
            gram_all.at[own], gram_all.at[own], g_send.at[dz * n + dd], g_recv.at[own],
            dom=lax.rem(me + dd, n), shift=lax.rem(group + dz, groups),
        )

    def shared(t):
        slot = lax.rem(own + t, groups * n)
        return remote(
            gram_all.at[slot], gram_all.at[slot], g_send.at[t], g_recv.at[slot],
            dom=right, shift=group,
        )

    def every(act):
        def one(t, carry):
            act(share(t // n, lax.rem(t, n)))
            return carry

        lax.fori_loop(1, groups * n, one, 0)

    every(lambda copy: copy.start())
    for i in range(2, groups):
        forward(i)
    for i in range(1, groups):
        settled(i)
        images_of(other(i))

    def wait_shared(t, carry):
        shared(t).wait_recv()
        return carry

    lax.fori_loop(1, groups * n, wait_shared, 0)
    for t in range(groups * n):
        gram_rows[t : t + 1] = gram_all[t]
    tau = jnp.zeros((1, LANES), jnp.float32)
    lane_row = lax.broadcasted_iota(jnp.int32, (1, LANES), 1)
    for j in range(shifts):
        tau = jnp.where(lane_row == j, table_ref[ids_ref[j]] - MID, tau)
    count = groups * nb
    grams = gram_rows[...]
    if n > nb:
        grams = jnp.sum(grams.reshape(groups, n // nb, nb, LANES), axis=1).reshape(count, LANES)
    for q, value in enumerate(weights(coefficients(grams, tau), tau)):
        for j in range(shifts):
            c_ref[q * shifts + j] = jnp.broadcast_to(value[:, j : j + 1], (count, LANES))

    @pl.when(has_right)
    def _():
        halo(group, 0).wait_send()
        for i in range(1, groups):
            halo(other(i), 0).wait_send()
        for which in range(2):
            coeff_halo(which, 0).wait_send()

    @pl.when(has_left)
    def _():
        halo(group, 1).wait_send()
        for i in range(1, groups):
            halo(other(i), 1).wait_send()
        for which in range(2):
            coeff_halo(which, 1).wait_send()

    for i in range(groups):
        slot = other(i)

        @pl.when(up_from(slot))
        def _():
            across(slot, 0).wait_send()

        @pl.when(down_from(slot))
        def _():
            across(slot, 1).wait_send()

    def sent(u, carry):
        each_target(u, lambda copy: copy.wait_send())
        return carry

    lax.fori_loop(0, steps, sent, 0)
    every(lambda copy: copy.wait_send())


def combine_kernel(image_ref, c_ref, sol_ref, res_ref):
    shifts, batch = sol_ref.shape[0], sol_ref.shape[1]
    first = pl.program_id(0) * batch

    def one_source(i, carry):
        b = first + i
        w0 = image_ref[0, b]
        for j in range(shifts):
            z0 = image_ref[1 + j, b]
            z1 = image_ref[1 + shifts + j, b]
            z2 = image_ref[1 + 2 * shifts + j, b]
            of_w0, of_z0, of_z1, c0, c1, c2 = [
                c_ref[q * shifts + j, pl.ds(b, 1)] for q in range(WEIGHTS)
            ]
            sol_ref[j, i] = of_w0 * w0 + of_z0 * z0 + of_z1 * z1
            res_ref[j, i] = w0 - c0 * z0 - c1 * z1 - c2 * z2
        return carry

    lax.fori_loop(0, batch, one_source, 0)


def on_device(sources, kappa, mass, shift_table, shift_ids, sketch):
    n, groups = lax.axis_size("dom"), lax.axis_size("shift")
    nb, slab = sources.shape[0], sources.shape[1]
    tail = sources.shape[2:]
    shifts = shift_ids.shape[0]
    rows = sketch.shape[0]
    block = rows // 8
    cells = slab * tail[0] * tail[1]
    planes = slab + 2 * HALO
    count = groups * nb
    columns = BASIS * nb
    stride = rows // STEPS
    parts = stride // LANES
    chunk = rows // (n // nb)
    turns = chunk // stride
    vmem = pl.BlockSpec(memory_space=pltpu.VMEM)
    hbm = pl.BlockSpec(memory_space=pl.ANY)
    smem = pl.BlockSpec(memory_space=pltpu.SMEM)
    dma = pltpu.SemaphoreType.DMA
    f32 = jnp.float32
    images, solved = pl.pallas_call(
        functools.partial(project_kernel, n, groups),
        out_shape=(
            pltpu.VMEM((1 + 3 * shifts, count, slab) + tail, f32),
            pltpu.VMEM((WEIGHTS * shifts, count, LANES), f32),
        ),
        in_specs=[hbm, hbm, hbm, smem, smem, hbm],
        out_specs=(vmem, vmem),
        scratch_shapes=[
            pltpu.VMEM((groups, nb, planes) + tail, f32),
            pltpu.VMEM((2, planes) + tail, f32),
            pltpu.VMEM((rows // block, block, slab) + tail, jnp.bfloat16),
            pltpu.VMEM((rows, cells), jnp.bfloat16),
            pltpu.VMEM((2 * columns, slab) + tail, jnp.bfloat16),
            pltpu.VMEM((2 * columns, cells), jnp.bfloat16),
            pltpu.VMEM((STEPS, columns, parts, 1, LANES), f32),
            pltpu.VMEM((n, BASIS, turns * parts, 1, LANES), f32),
            pltpu.VMEM((BASIS, turns * parts, LANES), f32),
            pltpu.VMEM((groups * n, 1, LANES), f32),
            pltpu.VMEM((groups * n, LANES), f32),
            dma((rows // block,)), dma((3,)),
            dma((groups, 2)), dma((groups,)),
            dma((groups, 2)), dma((groups, 2)),
            dma((2, 2)), dma((2, 2)),
            dma((STEPS, nb)), dma((n, turns)),
            dma((groups * n,)), dma((groups * n,)),
        ],
        compiler_params=pltpu.CompilerParams(
            collective_id=0, has_side_effects=True, vmem_limit_bytes=46 << 20
        ),
        name="project",
    )(sources, kappa, mass, shift_table, shift_ids, sketch)

    batch = 4 if count % 4 == 0 else 1
    out = jax.ShapeDtypeStruct((shifts, count, slab) + tail, f32)
    out_spec = pl.BlockSpec((shifts, batch, slab) + tail, lambda i: (0, i, 0, 0, 0))
    return pl.pallas_call(
        combine_kernel,
        grid=(count // batch,),
        out_shape=(out, out),
        in_specs=[vmem, vmem],
        out_specs=(out_spec, out_spec),
        compiler_params=pltpu.CompilerParams(vmem_limit_bytes=32 << 20),
        name="combine",
    )(
        pltpu.with_memory_space_constraint(images, pltpu.VMEM),
        pltpu.with_memory_space_constraint(solved, pltpu.VMEM),
    )


def solution(mesh):
    placed = (
        P("shift", "dom", None, None),
        P("dom", None, None),
        P("dom", None, None),
        P(),
        P("shift"),
        P(None, "dom", None, None),
    )
    return jax.shard_map(
        on_device,
        mesh=mesh,
        in_specs=placed,
        out_specs=(P("shift", None, "dom", None, None), P("shift", None, "dom", None, None)),
        check_vma=False,
    )
```

time: 59.1 us -> 60.2 us (1.019)
  Pallas kernels: 58.3 us -> 59.4 us
    pallas_call x1, Pallas kernels: 43.4 us -> 54.3 us  [on_device(): pl.pallas_call(functools.partial(project_kernel, n, groups), out_shape=(p...]
    pallas_call x1, Pallas kernels: 14.9 us -> 5.09 us  [on_device(): pl.pallas_call(combine_kernel, grid=(count // batch,), out_shape=(out, ou...]
where the time goes in v1:
time: 60.2 us; the launch traced here: 60 us
  Pallas kernels  59.4 us (99%)
  between operations  0.64 us (1%)
    pallas_call x1, Pallas kernels, on_device(): pl.pallas_call(functools.partial(project_kernel, n, groups), out_shape=(p...  54.3 us
    pallas_call x1, Pallas kernels, on_device(): pl.pallas_call(combine_kernel, grid=(count // batch,), out_shape=(out, ou...  5.09 us

profile of v1, /device:TPU:1, one launch (start us, length us, event | category | flops | bytes accessed | tf_op | source)
XLA Modules:
  0.0 60.0 jit_solution(3945979993156087938)
XLA Ops:
  0.6 54.3 %project.1 = (f32[13,32,4,16,128]{4,3,2,1,0:T(8,128)S(1)}, f32[24,32,128]{2,1,0:T(8,128)S(1)}) custom-call(f32[8,4,16,128]{3,2,1,0:T(8,128)} %src_hbm.1, f32[4,16,128]{2,1,0:T(8,128)} %kappa_hbm.1, f32[4,16,128]{2,1,0:T(8,128)} %mass_hbm.1, f32[64]{0:T(128)} %table_ref.1, s32[4]{0:T(128)} %ids_ref.1, bf16[1024,4,16,128]{3,2,1,0:T(8,128)(2,1)} %sketch_ref.1), custom_call_target="tpu_custom_call" | custom-call | tf_op jit(solution)/shard_map/project/pallas_call | solution.py:536
  55.0 5.1 %combine.1 = (f32[4,32,4,16,128]{4,3,2,1,0:T(8,128)}, f32[4,32,4,16,128]{4,3,2,1,0:T(8,128)}) custom-call(f32[13,32,4,16,128]{4,3,2,1,0:T(8,128)S(1)} %get-tuple-element.4.image_ref, f32[24,32,128]{2,1,0:T(8,128)S(1)} %get-tuple-element.5.c_ref), custom_call_target="tpu_custom_call" | custom-call | tf_op jit(solution)/shard_map/combine/pallas_call | solution.py:572

commit v2 on v1

--- a/solution.py
+++ b/solution.py
@@ -9,6 +9,8 @@
 
 HALO = 3
 STEPS = 4
+HALVES = 2
+EARLY = 3
 LANES = 128
 MID = 2.25
 BASIS = 10
@@ -193,6 +195,14 @@
         )
         coeff_ref[:, pl.ds(slab + HALO, HALO)] = jnp.zeros((2, HALO) + tail, jnp.float32)
 
+    def settle(t, carry):
+        load(t).wait()
+        mat_ref[pl.ds(pl.multiple_of(t * block, block), block)] = rows_buf[t].reshape(
+            block, mat_ref.shape[1]
+        )
+        return carry
+
+    lax.fori_loop(0, EARLY, settle, 0)
     for copy in arguments:
         copy.wait()
     pl.semaphore_wait(barrier, n - 1 + groups - 1)
@@ -202,11 +212,12 @@
             return pl.ds(slab, HALO), pl.ds(0, HALO), right
         return pl.ds(HALO, HALO), pl.ds(slab + HALO, HALO), left
 
-    def halo(slot, side):
+    def halo(slot, side, part):
         first, target, there = sides(side)
+        some = pl.ds(part * (nb // HALVES), nb // HALVES)
         return remote(
-            wide_ref.at[slot, :, first], wide_ref.at[slot, :, target],
-            halo_send.at[slot, side], halo_recv.at[slot, side], dom=there,
+            wide_ref.at[slot, some, first], wide_ref.at[slot, some, target],
+            halo_send.at[slot, side, part], halo_recv.at[slot, side, part], dom=there,
         )
 
     def coeff_halo(which, side):
@@ -245,13 +256,15 @@
 
     @pl.when(has_right)
     def _():
-        halo(group, 0).start()
+        for part in range(HALVES):
+            halo(group, 0, part).start()
         for which in range(2):
             coeff_halo(which, 0).start()
 
     @pl.when(has_left)
     def _():
-        halo(group, 1).start()
+        for part in range(HALVES):
+            halo(group, 1, part).start()
         for which in range(2):
             coeff_halo(which, 1).start()
 
@@ -263,30 +276,34 @@
     def _():
         across(group, 1).start()
 
-    def settle(t, carry):
-        load(t).wait()
-        mat_ref[pl.ds(pl.multiple_of(t * block, block), block)] = rows_buf[t].reshape(
-            block, mat_ref.shape[1]
-        )
-        return carry
-
-    lax.fori_loop(0, blocks, settle, 0)
+    lax.fori_loop(EARLY, blocks, settle, 0)
 
     @pl.when(has_left)
     def _():
-        halo(group, 0).wait_recv()
+        for part in range(HALVES):
+            halo(group, 0, part).wait_recv()
         for which in range(2):
             coeff_halo(which, 0).wait_recv()
 
     @pl.when(has_right)
     def _():
-        halo(group, 1).wait_recv()
+        for part in range(HALVES):
+            halo(group, 1, part).wait_recv()
         for which in range(2):
             coeff_halo(which, 1).wait_recv()
 
-    def forward(i):
+    half = nb // HALVES
+
+    def relayed(slot):
+        below = jnp.logical_and(slot < group, has_up)
+        return jnp.logical_or(below, jnp.logical_and(slot > group, has_down))
+
+    def pass_on(i):
         slot = other(i)
-        across(slot, 0).wait_recv()
+
+        @pl.when(relayed(slot))
+        def _():
+            across(slot, 0).wait_recv()
 
         @pl.when(up_from(slot))
         def _():
@@ -296,25 +313,34 @@
         def _():
             across(slot, 1).start()
 
+    def spread_planes(i):
+        slot = other(i)
+
+        @pl.when(jnp.logical_not(relayed(slot)))
+        def _():
+            across(slot, 0).wait_recv()
+
+        for part in range(HALVES):
+            @pl.when(has_right)
+            def _():
+                halo(slot, 0, part).start()
+
+            @pl.when(has_left)
+            def _():
+                halo(slot, 1, part).start()
+
+    def settled(slot, part):
+        @pl.when(has_left)
+        def _():
+            halo(slot, 0, part).wait_recv()
+
         @pl.when(has_right)
         def _():
-            halo(slot, 0).start()
-
-        @pl.when(has_left)
-        def _():
-            halo(slot, 1).start()
-
-    def settled(i):
-        slot = other(i)
-
-        @pl.when(has_left)
-        def _():
-            halo(slot, 0).wait_recv()
-
-        @pl.when(has_right)
-        def _():
-            halo(slot, 1).wait_recv()
-
+            halo(slot, 1, part).wait_recv()
+
+    for i in range(1, min(groups, 3)):
+        pass_on(i)
+    spread_planes(1)
     low, high = edge_flags()
     planes = slab + 2 * HALO
 
@@ -337,7 +363,7 @@
     lax.fori_loop(0, nb, one_source, 0)
     fields_ref[...] = raw_ref[...].reshape(fields_ref.shape)
 
-    def images_of(slot):
+    def images_of(slot, part):
         def one(b, carry):
             w0, a0, a1, b0, b1, b2, e0, e1, e2, e3 = basis_of(slot, b)
             place = slot * nb + b
@@ -349,21 +375,14 @@
                 image_ref[1 + 2 * shifts + j, place] = e0 + tau * (e1 + tau * (e2 + tau * e3))
             return carry
 
-        lax.fori_loop(0, nb, one, 0)
+        lax.fori_loop(part * half, (part + 1) * half, one, 0)
 
     def scatter(u, there):
         turn = lax.rem(u, turns)
         return remote(
             out_buf.at[u, pl.ds(lax.rem(there, nb) * BASIS, BASIS)],
             in_buf.at[me, :, pl.ds(turn * parts, parts)],
-            rs_send.at[u, lax.rem(there, nb)], rs_recv.at[me, turn], dom=there,
-        )
-
-    def gathered(source, turn):
-        return remote(
-            out_buf.at[turn, pl.ds(0, BASIS)],
-            in_buf.at[source, :, pl.ds(turn * parts, parts)],
-            rs_send.at[turn, 0], rs_recv.at[source, turn], dom=source,
+            rs_send.at[u, lax.rem(there, nb)], rs_recv, dom=there,
         )
 
     def each_target(u, act):
@@ -387,17 +406,24 @@
         each_target(u, lambda copy: copy.start())
         return carry
 
-    lax.fori_loop(0, steps, step, 0)
-    forward(1)
-    images_of(group)
+    lax.fori_loop(0, steps // 2, step, 0)
+    for i in range(3, groups):
+        pass_on(i)
+    lax.fori_loop(steps // 2, steps, step, 0)
+    spread_planes(2)
+    for part in range(HALVES):
+        images_of(group, part)
+    for part in range(HALVES):
+        settled(other(1), part)
+        images_of(other(1), part)
 
     first_turn = (me // nb) * turns
     mine = pl.ds(lax.rem(me, nb) * BASIS, BASIS)
     for turn in range(turns):
         in_buf[me, :, pl.ds(turn * parts, parts)] = out_buf[first_turn + turn, mine]
-    for t in range(1, n):
-        for turn in range(turns):
-            gathered(lax.rem(me + t, n), turn).wait_recv()
+    remote(
+        in_buf.at[pl.ds(0, n - 1)], in_buf.at[pl.ds(0, n - 1)], rs_send.at[0, 0], rs_recv, dom=right
+    ).wait_recv()
     for k in range(BASIS):
         summed = in_buf[0, k]
         for source in range(1, n):
@@ -411,38 +437,29 @@
     own = group * n + me
     gram_all[own] = jnp.sum(gram, axis=0, keepdims=True)
 
-    def share(dz, dd):
-        return remote(
-            gram_all.at[own], gram_all.at[own], g_send.at[dz * n + dd], g_recv.at[own],
-            dom=lax.rem(me + dd, n), shift=lax.rem(group + dz, groups),
-        )
-
-    def shared(t):
-        slot = lax.rem(own + t, groups * n)
-        return remote(
-            gram_all.at[slot], gram_all.at[slot], g_send.at[t], g_recv.at[slot],
-            dom=right, shift=group,
-        )
-
     def every(act):
-        def one(t, carry):
-            act(share(t // n, lax.rem(t, n)))
-            return carry
-
-        lax.fori_loop(1, groups * n, one, 0)
-
-    every(lambda copy: copy.start())
+        for dz in range(groups - 1, -1, -1):
+            there = lax.rem(group + dz, groups)
+            for dd in range(n):
+                if dz or dd:
+                    act(there, lax.rem(me + dd, n))
+
+    def share(there, where):
+        remote(
+            gram_all.at[own], gram_all.at[own], g_send, g_recv, dom=where, shift=there
+        ).start()
+
+    others = gram_all.at[pl.ds(0, groups * n - 1)]
+    everybody = remote(others, others, g_send, g_recv, dom=right)
+    every(share)
+    for i in range(3, groups):
+        spread_planes(i)
     for i in range(2, groups):
-        forward(i)
-    for i in range(1, groups):
-        settled(i)
-        images_of(other(i))
-
-    def wait_shared(t, carry):
-        shared(t).wait_recv()
-        return carry
-
-    lax.fori_loop(1, groups * n, wait_shared, 0)
+        for part in range(HALVES):
+            settled(other(i), part)
+            images_of(other(i), part)
+
+    everybody.wait_recv()
     for t in range(groups * n):
         gram_rows[t : t + 1] = gram_all[t]
     tau = jnp.zeros((1, LANES), jnp.float32)
@@ -459,17 +476,17 @@
 
     @pl.when(has_right)
     def _():
-        halo(group, 0).wait_send()
-        for i in range(1, groups):
-            halo(other(i), 0).wait_send()
+        for i in range(groups):
+            for part in range(HALVES):
+                halo(other(i), 0, part).wait_send()
         for which in range(2):
             coeff_halo(which, 0).wait_send()
 
     @pl.when(has_left)
     def _():
-        halo(group, 1).wait_send()
-        for i in range(1, groups):
-            halo(other(i), 1).wait_send()
+        for i in range(groups):
+            for part in range(HALVES):
+                halo(other(i), 1, part).wait_send()
         for which in range(2):
             coeff_halo(which, 1).wait_send()
 
@@ -489,7 +506,7 @@
         return carry
 
     lax.fori_loop(0, steps, sent, 0)
-    every(lambda copy: copy.wait_send())
+    everybody.wait_send()
 
 
 def combine_kernel(image_ref, c_ref, sol_ref, res_ref):
@@ -555,10 +572,10 @@
             pltpu.VMEM((groups * n, LANES), f32),
             dma((rows // block,)), dma((3,)),
             dma((groups, 2)), dma((groups,)),
-            dma((groups, 2)), dma((groups, 2)),
+            dma((groups, 2, HALVES)), dma((groups, 2, HALVES)),
             dma((2, 2)), dma((2, 2)),
-            dma((STEPS, nb)), dma((n, turns)),
-            dma((groups * n,)), dma((groups * n,)),
+            dma((STEPS, nb)), dma,
+            dma, dma,
         ],
         compiler_params=pltpu.CompilerParams(
             collective_id=0, has_side_effects=True, vmem_limit_bytes=46 << 20

time: 60.2 us -> 44.5 us (0.74)
  Pallas kernels: 59.4 us -> 43.7 us
    pallas_call x1, Pallas kernels: 54.3 us -> 38.6 us  [on_device(): pl.pallas_call(functools.partial(project_kernel, n, groups), out_shape=(p...]
where the time goes in v2:
time: 44.5 us; the launch traced here: 44.4 us
  Pallas kernels  43.7 us (98%)
  between operations  0.64 us (1%)
    pallas_call x1, Pallas kernels, on_device(): pl.pallas_call(functools.partial(project_kernel, n, groups), out_shape=(p...  38.6 us
    pallas_call x1, Pallas kernels, on_device(): pl.pallas_call(combine_kernel, grid=(count // batch,), out_shape=(out, ou...  5.09 us

profile of v2, /device:TPU:1, one launch (start us, length us, event | category | flops | bytes accessed | tf_op | source)
XLA Modules:
  0.0 44.4 jit_solution(7292706767896591887)
XLA Ops:
  0.6 38.6 %project.1 = (f32[13,32,4,16,128]{4,3,2,1,0:T(8,128)S(1)}, f32[24,32,128]{2,1,0:T(8,128)S(1)}) custom-call(f32[8,4,16,128]{3,2,1,0:T(8,128)} %src_hbm.1, f32[4,16,128]{2,1,0:T(8,128)} %kappa_hbm.1, f32[4,16,128]{2,1,0:T(8,128)} %mass_hbm.1, f32[64]{0:T(128)} %table_ref.1, s32[4]{0:T(128)} %ids_ref.1, bf16[1024,4,16,128]{3,2,1,0:T(8,128)(2,1)} %sketch_ref.1), custom_call_target="tpu_custom_call" | custom-call | tf_op jit(solution)/shard_map/project/pallas_call | solution.py:553
  39.3 5.1 %combine.1 = (f32[4,32,4,16,128]{4,3,2,1,0:T(8,128)}, f32[4,32,4,16,128]{4,3,2,1,0:T(8,128)}) custom-call(f32[13,32,4,16,128]{4,3,2,1,0:T(8,128)S(1)} %get-tuple-element.4.image_ref, f32[24,32,128]{2,1,0:T(8,128)S(1)} %get-tuple-element.5.c_ref), custom_call_target="tpu_custom_call" | custom-call | tf_op jit(solution)/shard_map/combine/pallas_call | solution.py:589

commit v3 on v2

--- a/solution.py
+++ b/solution.py
@@ -227,10 +227,11 @@
             km_recv.at[which, side], dom=there,
         )
 
-    def across(slot, way):
+    def across(slot, way, part):
+        some = pl.ds(part * (nb // HALVES), nb // HALVES)
         return remote(
-            wide_ref.at[slot, :, inner], wide_ref.at[slot, :, inner],
-            z_send.at[slot, way], z_recv.at[slot],
+            wide_ref.at[slot, some, inner], wide_ref.at[slot, some, inner],
+            z_send.at[slot, way, part], z_recv.at[slot, part],
             shift=group + 1 - 2 * way,
         )
 
@@ -256,39 +257,37 @@
 
     @pl.when(has_right)
     def _():
+        for which in range(2):
+            coeff_halo(which, 0).start()
         for part in range(HALVES):
             halo(group, 0, part).start()
+
+    @pl.when(has_left)
+    def _():
         for which in range(2):
-            coeff_halo(which, 0).start()
-
-    @pl.when(has_left)
-    def _():
+            coeff_halo(which, 1).start()
         for part in range(HALVES):
             halo(group, 1, part).start()
-        for which in range(2):
-            coeff_halo(which, 1).start()
 
     @pl.when(has_up)
     def _():
-        across(group, 0).start()
+        for part in range(HALVES):
+            across(group, 0, part).start()
 
     @pl.when(has_down)
     def _():
-        across(group, 1).start()
+        for part in range(HALVES):
+            across(group, 1, part).start()
 
     lax.fori_loop(EARLY, blocks, settle, 0)
 
     @pl.when(has_left)
     def _():
-        for part in range(HALVES):
-            halo(group, 0, part).wait_recv()
         for which in range(2):
             coeff_halo(which, 0).wait_recv()
 
     @pl.when(has_right)
     def _():
-        for part in range(HALVES):
-            halo(group, 1, part).wait_recv()
         for which in range(2):
             coeff_halo(which, 1).wait_recv()
 
@@ -301,26 +300,27 @@
     def pass_on(i):
         slot = other(i)
 
-        @pl.when(relayed(slot))
-        def _():
-            across(slot, 0).wait_recv()
-
-        @pl.when(up_from(slot))
-        def _():
-            across(slot, 0).start()
-
-        @pl.when(down_from(slot))
-        def _():
-            across(slot, 1).start()
+        for part in range(HALVES):
+            @pl.when(relayed(slot))
+            def _():
+                across(slot, 0, part).wait_recv()
+
+            @pl.when(up_from(slot))
+            def _():
+                across(slot, 0, part).start()
+
+            @pl.when(down_from(slot))
+            def _():
+                across(slot, 1, part).start()
 
     def spread_planes(i):
         slot = other(i)
 
-        @pl.when(jnp.logical_not(relayed(slot)))
-        def _():
-            across(slot, 0).wait_recv()
-
         for part in range(HALVES):
+            @pl.when(jnp.logical_not(relayed(slot)))
+            def _():
+                across(slot, 0, part).wait_recv()
+
             @pl.when(has_right)
             def _():
                 halo(slot, 0, part).start()
@@ -338,9 +338,6 @@
         def _():
             halo(slot, 1, part).wait_recv()
 
-    for i in range(1, min(groups, 3)):
-        pass_on(i)
-    spread_planes(1)
     low, high = edge_flags()
     planes = slab + 2 * HALO
 
@@ -360,7 +357,13 @@
             )
         return carry
 
-    lax.fori_loop(0, nb, one_source, 0)
+    for part in range(HALVES):
+        settled(group, part)
+        if part == HALVES - 1:
+            for i in range(1, min(groups, 3)):
+                pass_on(i)
+            spread_planes(1)
+        lax.fori_loop(part * half, (part + 1) * half, one_source, 0)
     fields_ref[...] = raw_ref[...].reshape(fields_ref.shape)
 
     def images_of(slot, part):
@@ -406,16 +409,15 @@
         each_target(u, lambda copy: copy.start())
         return carry
 
-    lax.fori_loop(0, steps // 2, step, 0)
+    lax.fori_loop(0, steps - 1, step, 0)
     for i in range(3, groups):
         pass_on(i)
-    lax.fori_loop(steps // 2, steps, step, 0)
+    lax.fori_loop(steps - 1, steps, step, 0)
     spread_planes(2)
     for part in range(HALVES):
         images_of(group, part)
-    for part in range(HALVES):
-        settled(other(1), part)
-        images_of(other(1), part)
+    settled(other(1), 0)
+    images_of(other(1), 0)
 
     first_turn = (me // nb) * turns
     mine = pl.ds(lax.rem(me, nb) * BASIS, BASIS)
@@ -454,6 +456,27 @@
     every(share)
     for i in range(3, groups):
         spread_planes(i)
+    def sent(u, carry):
+        each_target(u, lambda copy: copy.wait_send())
+        return carry
+
+    lax.fori_loop(0, steps, sent, 0)
+
+    for i in range(groups):
+        slot = other(i)
+
+        @pl.when(up_from(slot))
+        def _():
+            for part in range(HALVES):
+                across(slot, 0, part).wait_send()
+
+        @pl.when(down_from(slot))
+        def _():
+            for part in range(HALVES):
+                across(slot, 1, part).wait_send()
+
+    settled(other(1), 1)
+    images_of(other(1), 1)
     for i in range(2, groups):
         for part in range(HALVES):
             settled(other(i), part)
@@ -490,31 +513,21 @@
         for which in range(2):
             coeff_halo(which, 1).wait_send()
 
-    for i in range(groups):
-        slot = other(i)
-
-        @pl.when(up_from(slot))
-        def _():
-            across(slot, 0).wait_send()
-
-        @pl.when(down_from(slot))
-        def _():
-            across(slot, 1).wait_send()
-
-    def sent(u, carry):
-        each_target(u, lambda copy: copy.wait_send())
-        return carry
-
-    lax.fori_loop(0, steps, sent, 0)
     everybody.wait_send()
 
 
-def combine_kernel(image_ref, c_ref, sol_ref, res_ref):
-    shifts, batch = sol_ref.shape[0], sol_ref.shape[1]
-    first = pl.program_id(0) * batch
-
-    def one_source(i, carry):
-        b = first + i
+def combine_kernel(image_ref, c_ref, sol_hbm, res_hbm, sol_ref, res_ref, sem):
+    shifts, count = sol_ref.shape[0], sol_ref.shape[1]
+    batch = count // sem.shape[1]
+
+    def leave(k):
+        part = pl.ds(k * batch, batch)
+        return [
+            pltpu.make_async_copy(here.at[:, part], there.at[:, part], sem.at[which, k])
+            for which, (here, there) in enumerate(((sol_ref, sol_hbm), (res_ref, res_hbm)))
+        ]
+
+    def one_source(b, carry):
         w0 = image_ref[0, b]
         for j in range(shifts):
             z0 = image_ref[1 + j, b]
@@ -523,11 +536,23 @@
             of_w0, of_z0, of_z1, c0, c1, c2 = [
                 c_ref[q * shifts + j, pl.ds(b, 1)] for q in range(WEIGHTS)
             ]
-            sol_ref[j, i] = of_w0 * w0 + of_z0 * z0 + of_z1 * z1
-            res_ref[j, i] = w0 - c0 * z0 - c1 * z1 - c2 * z2
+            sol_ref[j, b] = of_w0 * w0 + of_z0 * z0 + of_z1 * z1
+            res_ref[j, b] = w0 - c0 * z0 - c1 * z1 - c2 * z2
         return carry
 
-    lax.fori_loop(0, batch, one_source, 0)
+    def one_batch(k, carry):
+        lax.fori_loop(k * batch, (k + 1) * batch, one_source, 0)
+        for copy in leave(k):
+            copy.start()
+        return carry
+
+    def gone(k, carry):
+        for copy in leave(k):
+            copy.wait()
+        return carry
+
+    lax.fori_loop(0, sem.shape[1], one_batch, 0)
+    lax.fori_loop(0, sem.shape[1], gone, 0)
 
 
 def on_device(sources, kappa, mass, shift_table, shift_ids, sketch):
@@ -571,7 +596,7 @@
             pltpu.VMEM((groups * n, 1, LANES), f32),
             pltpu.VMEM((groups * n, LANES), f32),
             dma((rows // block,)), dma((3,)),
-            dma((groups, 2)), dma((groups,)),
+            dma((groups, 2, HALVES)), dma((groups, HALVES)),
             dma((groups, 2, HALVES)), dma((groups, 2, HALVES)),
             dma((2, 2)), dma((2, 2)),
             dma((STEPS, nb)), dma,
@@ -583,16 +608,20 @@
         name="project",
     )(sources, kappa, mass, shift_table, shift_ids, sketch)
 
-    batch = 4 if count % 4 == 0 else 1
-    out = jax.ShapeDtypeStruct((shifts, count, slab) + tail, f32)
-    out_spec = pl.BlockSpec((shifts, batch, slab) + tail, lambda i: (0, i, 0, 0, 0))
+    batch = 2 if count % 2 == 0 else 1
+    everything = (shifts, count, slab) + tail
+    out = pltpu.HBM(everything, f32)
     return pl.pallas_call(
         combine_kernel,
-        grid=(count // batch,),
         out_shape=(out, out),
         in_specs=[vmem, vmem],
-        out_specs=(out_spec, out_spec),
-        compiler_params=pltpu.CompilerParams(vmem_limit_bytes=32 << 20),
+        out_specs=(pl.BlockSpec(memory_space=pltpu.HBM),) * 2,
+        scratch_shapes=[
+            pltpu.VMEM(everything, f32),
+            pltpu.VMEM(everything, f32),
+            dma((2, count // batch)),
+        ],
+        compiler_params=pltpu.CompilerParams(vmem_limit_bytes=20 << 20),
         name="combine",
     )(
         pltpu.with_memory_space_constraint(images, pltpu.VMEM),

time: 44.5 us -> 42 us (0.944); the launches traced: 44.4 us -> 41.3 us
  Pallas kernels: 43.7 us -> 40.7 us
    pallas_call x1, Pallas kernels: 38.6 us -> 37 us  [on_device(): pl.pallas_call(functools.partial(project_kernel, n, groups), out_shape=(p...]
    pallas_call x1, Pallas kernels: 5.09 us -> 3.65 us  [on_device(): pl.pallas_call(combine_kernel, out_shape=(out, out), in_specs=[vmem, vmem...]
where the time goes in v3:
time: 42 us; the launch traced here: 41.3 us
  Pallas kernels  40.7 us (97%)
  between operations  0.64 us (2%)
    pallas_call x1, Pallas kernels, on_device(): pl.pallas_call(functools.partial(project_kernel, n, groups), out_shape=(p...  37 us
    pallas_call x1, Pallas kernels, on_device(): pl.pallas_call(combine_kernel, out_shape=(out, out), in_specs=[vmem, vmem...  3.65 us

profile of v3, /device:TPU:1, one launch (start us, length us, event | category | flops | bytes accessed | tf_op | source)
XLA Modules:
  0.0 41.3 jit_solution(12237186197432900494)
XLA Ops:
  0.6 37.0 %project.1 = (f32[13,32,4,16,128]{4,3,2,1,0:T(8,128)S(1)}, f32[24,32,128]{2,1,0:T(8,128)S(1)}) custom-call(f32[8,4,16,128]{3,2,1,0:T(8,128)} %src_hbm.1, f32[4,16,128]{2,1,0:T(8,128)} %kappa_hbm.1, f32[4,16,128]{2,1,0:T(8,128)} %mass_hbm.1, f32[64]{0:T(128)} %table_ref.1, s32[4]{0:T(128)} %ids_ref.1, bf16[1024,4,16,128]{3,2,1,0:T(8,128)(2,1)} %sketch_ref.1), custom_call_target="tpu_custom_call" | custom-call | tf_op jit(solution)/shard_map/project/pallas_call | solution.py:578
  37.7 3.6 %combine.1 = (f32[4,32,4,16,128]{4,3,2,1,0:T(8,128)}, f32[4,32,4,16,128]{4,3,2,1,0:T(8,128)}) custom-call(f32[13,32,4,16,128]{4,3,2,1,0:T(8,128)S(1)} %get-tuple-element.4.image_ref, f32[24,32,128]{2,1,0:T(8,128)S(1)} %get-tuple-element.5.c_ref), custom_call_target="tpu_custom_call" | custom-call | tf_op jit(solution)/shard_map/combine/pallas_call | solution.py:614
